TPU v7x, 32 devices: a whole 2x2x4 slice. The times are simulated.
32 devices in a mesh: view: 4 (over x, core), depth: 8 (over z, y).
Axes of the slice: x: 2, y: 2, z: 4, core: 2. Of those that a mesh axis runs over, the one named last changes fastest.
Arguments:
- volume: float32 [128, 128, 512], P(('view', 'depth')), may hold values from -6 to 6
- step_weights: float32 [4, 8, 64], P('view'), may hold values from -0.75 to 0.75
- row_interp: float32 [4, 64, 64], P('view'), may hold values from -0.75 to 0.75
- col_interp: float32 [4, 64, 64], P('view'), may hold values from -0.75 to 0.75
- tf_table: float32 [8, 8], replicated, may hold values from -3 to 3
- materials: int32 [2, 2, 8], P(None, None, 'depth'), may hold values from 0 to 7
- entry: int32 [4, 128, 128], P('view'), may hold values from 0 to 3
Outputs:
- picture: float32 [4, 3, 128, 128], P('view', None, 'depth')
All inputs are finite; a program needn't handle non-finite values.
Results may differ from a plain program's by a relative error of at most 0.00018.
Values sent between devices are 32-bit elements; how exact they have to be, the bound alone decides.
No kernel may reach another device: no remote copies, remote signals or barrier semaphores. Data moves between devices by JAX's collectives and lax.ppermute only.
A program may use at most 64 MiB of HBM per device.

v0:
```python
import functools

import jax
import jax.numpy as jnp
from jax import lax
from jax.experimental import pallas as pl
from jax.experimental.pallas import tpu as pltpu
from jax.sharding import PartitionSpec as P


LANES = 128
SUB = 8
COEF = 8
HIGHEST = lax.Precision.HIGHEST
NT = (((1,), (1,)), ((), ()))
NN = (((1,), (0,)), ((), ()))


def split(x):
    hi = x.astype(jnp.bfloat16)
    return hi, (x - hi.astype(jnp.float32)).astype(jnp.bfloat16)


def softplus(v):
    e = jnp.exp(-jnp.abs(v))
    small = e * (1.0 - 0.5 * e)
    return jnp.maximum(v, 0.0) + jnp.where(e < 1e-4, small, jnp.log(1.0 + e))


def pack_kernel(steps_hbm, cols_hbm, out_ref, steps_ref, cols_ref, sems):
    copies = [
        pltpu.make_async_copy(cols_hbm, cols_ref, sems.at[0]),
        pltpu.make_async_copy(steps_hbm, steps_ref, sems.at[1]),
    ]
    for copy in copies:
        copy.start()
    for copy in copies:
        copy.wait()
    edge = cols_ref.shape[1]
    out_ref[0, : edge // 2] = jnp.concatenate([cols_ref[0, : edge // 2], cols_ref[0, edge // 2 :]], axis=1)
    out_ref[0, edge // 2 :] = jnp.concatenate([steps_ref[0], steps_ref[0]], axis=1)


def prepare_kernel(
    order, depth_ref, classes_hbm, table_hbm, vol_hbm, row_hbm, entry_hbm,
    hi_ref, lo_ref, maps_hi_ref, maps_lo_ref, entry_own_ref, coef_ref,
    classes_ref, table_ref, vol_ref, row_ref, entry_ref, turned_ref, moved_ref, sems,
):
    planes, lateral, _ = vol_ref.shape
    tiles_z, tiles_y = classes_ref.shape[0], classes_ref.shape[2]
    per = entry_own_ref.shape[0]
    pieces = [(vol_hbm.at[p], vol_ref.at[p]) for p in range(planes)]
    pieces += [(entry_hbm, entry_ref), (row_hbm, row_ref), (classes_hbm, classes_ref), (table_hbm, table_ref)]
    copies = [pltpu.make_async_copy(*piece, sems.at[n]) for n, piece in enumerate(pieces)]
    for copy in copies:
        copy.start()
    for copy in copies[planes:]:
        copy.wait()
    lane = lax.broadcasted_iota(jnp.int32, (1, LANES), 1)
    for u in range(tiles_y):
        row = jnp.zeros((1, LANES), jnp.float32)
        for t in range(tiles_z):
            for ch in range(COEF):
                row = jnp.where(lane == t * COEF + ch, table_ref[classes_ref[t, 0, u], ch], row)
        coef_ref[u : u + 1] = row
    turned = row_ref[0].T
    zero = jnp.zeros_like(turned)
    maps = jnp.concatenate(
        [jnp.concatenate([turned if i == t else zero for i in range(tiles_z)], axis=1) for t in range(tiles_z)],
        axis=0,
    )
    turned_ref[...] = maps
    for p in range(planes):
        for n, device in enumerate(order):
            to, at = p * len(order) + n, device * planes + p
            moved_ref[to : to + 1] = turned_ref[at : at + 1]
    maps_hi_ref[...], maps_lo_ref[...] = split(moved_ref[...])
    turned = entry_ref[0].astype(jnp.float32).T
    own = jnp.zeros((per, turned.shape[1]), jnp.float32)
    for d in range(turned.shape[0] // per):
        own = jnp.where(depth_ref[0] == d, turned[d * per : (d + 1) * per], own)
    entry_own_ref[...] = own.astype(jnp.int32)
    for p in range(planes):
        copies[p].wait()
        at = slice(p * lateral, (p + 1) * lateral)
        hi_ref[at], lo_ref[at] = split(vol_ref[p])


def send_kernel(order, depth, planes, pair, view_ref, hi_ref, lo_ref, coef_ref, *refs):
    out_ref = refs[-1]
    map_refs = refs[:2]
    edge = map_refs[0].shape[2] // 2
    lateral, span = hi_ref.shape[0] // planes, hi_ref.shape[1]
    bricks = span // edge
    per = lateral // depth
    block_rows = planes * SUB + 1
    views = len(order) // depth
    view = [view_ref[0] ^ (2 * pair + k) for k in range(2)]

    def first_row(k, d):
        row = order.index(d) * block_rows
        for v in range(1, views):
            row = jnp.where(view[k] == v, order.index(v * depth + d) * block_rows, row)
        return row

    starts = [[first_row(k, d) for d in range(depth)] for k in range(2)]

    weights = jnp.concatenate([ref[0, edge // 2 :] for ref in map_refs], axis=0)
    tiled = jnp.concatenate([weights] * (span // LANES), axis=1)
    lane = lax.broadcasted_iota(jnp.int32, (bricks, span), 1)
    brick = lax.broadcasted_iota(jnp.int32, (bricks, span), 0)
    own = lane // edge == brick
    ray = jnp.where(own[None], tiled[:, None, :], 0.0).reshape(weights.shape[0] * bricks, span)
    ray_hi, ray_lo = split(ray)
    both = lax.dot_general(
        hi_ref[...], jnp.concatenate([ray_hi, ray_lo], axis=0), NT, preferred_element_type=jnp.float32
    )
    first = both[:, :LANES] + (
        both[:, LANES:] + lax.dot_general(lo_ref[...], ray_hi, NT, preferred_element_type=jnp.float32)
    )
    first_hi, first_lo = split(first)

    half = lax.broadcasted_iota(jnp.int32, (SUB, LANES), 1) < edge
    left = lax.broadcasted_iota(jnp.int32, (edge // 2, LANES), 1) < edge
    rows = []
    for ref in map_refs:
        c = ref[0, : edge // 2]
        turned = pltpu.roll(c, edge, 1)
        rows += [jnp.where(left, c, 0.0), jnp.where(left, turned, 0.0)]
        rows += [jnp.where(left, 0.0, turned), jnp.where(left, 0.0, c)]
    maps_hi, maps_lo = split(jnp.concatenate(rows, axis=0))
    maps = jnp.concatenate([maps_hi, maps_lo], axis=1)
    for couple in range(planes // 2):
        at = [slice((2 * couple + i) * lateral, (2 * couple + i + 1) * lateral) for i in range(2)]
        high = jnp.concatenate([first_hi[i] for i in at], axis=1)
        low = jnp.concatenate([first_lo[i] for i in at], axis=1)
        second = lax.dot_general(
            maps, jnp.concatenate([high, high], axis=0), NN, preferred_element_type=jnp.float32
        ) + lax.dot_general(maps_hi, low, NN, preferred_element_type=jnp.float32)
        for i in range(2):
            plane = 2 * couple + i
            for k in range(2):
                for d in range(depth):
                    base = k * lateral + d * per
                    a = second[base : base + SUB, i * LANES : (i + 1) * LANES]
                    b = second[base + SUB : base + 2 * SUB, i * LANES : (i + 1) * LANES]
                    if k == 0:
                        b = pltpu.roll(b, edge, 1)
                    else:
                        a = pltpu.roll(a, edge, 1)
                    at_row = starts[k][d] + plane * SUB
                    out_ref[pl.ds(at_row, SUB), :] = jnp.where(half, a, b)
    for k in range(2):
        for d in range(depth):
            u = d * per // edge
            at_row = starts[k][d] + block_rows - 1
            out_ref[pl.ds(at_row, 1), :] = coef_ref[u : u + 1]


def render_kernel(step_length, planes, order, turn, recv_ref, maps_hi_ref, maps_lo_ref, entry_ref, out_ref):
    block_rows = planes * SUB + 1
    sources = recv_ref.shape[0] // block_rows
    columns, rows = entry_ref.shape
    bricks = steps = SUB
    maps_hi = maps_hi_ref[...]
    maps = jnp.concatenate([maps_hi, maps_hi], axis=0)
    maps_lo = maps_lo_ref[...]

    ends = [(order.index(b) + 1) * block_rows for b in range(bricks)]
    packed = jnp.concatenate([recv_ref[end - 1 : end] for end in ends], axis=0)
    lane = lax.broadcasted_iota(jnp.int32, (bricks, rows), 1)
    upper = lane >= rows // 2
    coef = []
    for ch in range(COEF):
        low = jnp.broadcast_to(packed[:, ch : ch + 1], (bricks, rows))
        high = jnp.broadcast_to(packed[:, COEF + ch : COEF + ch + 1], (bricks, rows))
        coef.append(jnp.where(upper, high, low))
    brick = lax.broadcasted_iota(jnp.int32, (bricks, rows), 0)

    shown = [[None] * columns for _ in range(3)]
    for x in range(SUB):
        cells = jnp.concatenate(
            [recv_ref[pl.ds(p * SUB + x, sources, stride=block_rows), :] for p in range(planes)], axis=0
        )
        high, low = split(cells.T)
        samples = lax.dot_general(
            jnp.concatenate([high, low], axis=1), maps, NN, preferred_element_type=jnp.float32
        ) + lax.dot_general(high, maps_lo, NN, preferred_element_type=jnp.float32)
        for m in range(2):
            c = m * SUB + x
            live = jnp.where(entry_ref[c : c + 1, :] <= brick, step_length, 0.0)
            total = jnp.zeros((bricks, rows), jnp.float32)
            before = jnp.ones((bricks, rows), jnp.float32)
            colours = [jnp.zeros((bricks, rows), jnp.float32) for _ in range(3)]
            for s in range(steps):
                at = (m * steps + s) * bricks
                v = samples[at : at + bricks]
                total = total + live * softplus(coef[6] * v + coef[7])
                after = jnp.exp(-total)
                weight = before - after
                before = after
                for ch in range(3):
                    colours[ch] = colours[ch] + weight * softplus(coef[ch] * v + coef[3 + ch])
            front = total
            for shift in (1, 2, 4):
                front = front + jnp.where(brick >= shift, pltpu.roll(front, shift, 0), 0.0)
            reach = jnp.exp(total - front)
            for ch in range(3):
                shown[ch][c] = jnp.sum(reach * colours[ch], axis=0, keepdims=True)
    blank = jnp.zeros((LANES // 2 - 3 * columns, rows), jnp.float32)
    image = jnp.concatenate([r for ch in shown for r in ch] + [blank], axis=0)
    image = jnp.concatenate([image, image], axis=0).T
    left = lax.broadcasted_iota(jnp.int32, (SUB, LANES), 1) < LANES // 2
    for n, d in enumerate(turn):
        at = d * 2 * SUB
        out_ref[n] = jnp.where(left, image[at : at + SUB], image[at + SUB : at + 2 * SUB])


def unpack_kernel(columns, turn, recv_ref, out_ref):
    owner = lax.broadcasted_iota(jnp.int32, (SUB, LANES), 1) // columns
    for ch in range(3):
        for h in range(2):
            out = jnp.zeros((SUB, LANES), jnp.float32)
            for n, s in enumerate(turn):
                moved = pltpu.roll(recv_ref[n], ((s - ch) * columns - h * (LANES // 2)) % LANES, 1)
                out = jnp.where(owner == s, moved, out)
            out_ref[0, ch, h * SUB : (h + 1) * SUB] = out


def small():
    return pltpu.CompilerParams(vmem_limit_bytes=16 * 1024 * 1024)


def orders(views, depth):
    order = [v * depth + z * 2 + y for y in range(2) for v in range(views) for z in range(depth // 2)]
    first = depth // 2 + 1
    return order, list(range(first, depth)) + list(range(first))


def vmem():
    return pl.BlockSpec(memory_space=pltpu.VMEM)


def hbm():
    return pl.BlockSpec(memory_space=pltpu.HBM)


def in_hbm(x):
    return pltpu.with_memory_space_constraint(x, pltpu.HBM)


def smem():
    return pl.BlockSpec(memory_space=pltpu.SMEM)


def with_kernels(volume, step_weights, row_interp, col_interp, tf_table, materials, entry):
    views = lax.axis_size("view")
    steps, edge = step_weights.shape[1:]
    depth = lax.axis_size("depth")
    planes, lateral, span = volume.shape
    devices = views * depth
    per = lateral // depth
    rows = devices * planes
    step_length = 2.0 / (steps * depth)
    tiles_y = lateral // edge
    block_rows = planes * SUB + 1
    order, turn = orders(views, depth)
    depth_at = lax.axis_index("depth").reshape(1)
    own = pl.pallas_call(
        pack_kernel,
        out_shape=jax.ShapeDtypeStruct((1, edge // 2 + steps, 2 * edge), jnp.float32),
        in_specs=[hbm()] * 2,
        out_specs=vmem(),
        scratch_shapes=[
            pltpu.VMEM(step_weights.shape, jnp.float32),
            pltpu.VMEM(col_interp.shape, jnp.float32),
            pltpu.SemaphoreType.DMA((2,)),
        ],
        compiler_params=small(),
        name="pack",
    )(in_hbm(step_weights), in_hbm(col_interp))
    maps = [own]
    for k in range(1, views):
        maps.append(lax.ppermute(own, "view", [(i, i ^ k) for i in range(views)]))
    hi, lo, maps_hi, maps_lo, entry_own, coef = pl.pallas_call(
        functools.partial(prepare_kernel, order),
        out_shape=[
            jax.ShapeDtypeStruct((planes * lateral, span), jnp.bfloat16),
            jax.ShapeDtypeStruct((planes * lateral, span), jnp.bfloat16),
            jax.ShapeDtypeStruct((rows, rows), jnp.bfloat16),
            jax.ShapeDtypeStruct((rows, rows), jnp.bfloat16),
            jax.ShapeDtypeStruct((per, rows), jnp.int32),
            jax.ShapeDtypeStruct((tiles_y, LANES), jnp.float32),
        ],
        in_specs=[smem()] + [hbm()] * 5,
        out_specs=[vmem()] * 6,
        scratch_shapes=[
            pltpu.SMEM((materials.shape[0], 1, tiles_y), jnp.int32),
            pltpu.SMEM(tf_table.shape, jnp.float32),
            pltpu.VMEM(volume.shape, jnp.float32),
            pltpu.VMEM(row_interp.shape, jnp.float32),
            pltpu.VMEM(entry.shape, jnp.int32),
            pltpu.VMEM((rows, rows), jnp.float32),
            pltpu.VMEM((rows, rows), jnp.float32),
            pltpu.SemaphoreType.DMA((planes + 4,)),
        ],
        compiler_params=small(),
        cost_estimate=pl.CostEstimate(flops=2_000_000_000, bytes_accessed=4_000_000, transcendentals=0),
        name="prepare",
    )(depth_at, *map(in_hbm, (materials.transpose(0, 2, 1), tf_table, volume, row_interp, entry)))
    view_at = lax.axis_index("view").reshape(1)
    blocks = []
    for pair in range(views // 2):
        blocks = [
            pl.pallas_call(
                functools.partial(send_kernel, order, depth, planes, pair),
                out_shape=jax.ShapeDtypeStruct((devices * block_rows, LANES), jnp.float32),
                in_specs=[smem()] + [vmem()] * (5 + len(blocks)),
                out_specs=vmem(),
                input_output_aliases={6: 0} if blocks else {},
                compiler_params=small(),
                cost_estimate=pl.CostEstimate(flops=1_000_000_000, bytes_accessed=2_000_000, transcendentals=0),
            )(view_at, hi, lo, coef, *maps[2 * pair : 2 * pair + 2], *blocks)
        ]
    blocks = blocks[0]
    blocks = blocks.reshape(devices, block_rows, 1, LANES)
    recv = lax.all_to_all(blocks, ("view", "depth"), split_axis=0, concat_axis=0, tiled=True, axis_index_groups=[order])
    recv = recv.reshape(devices * block_rows, LANES)
    image = pl.pallas_call(
        functools.partial(render_kernel, step_length, planes, order, turn),
        out_shape=jax.ShapeDtypeStruct((depth, SUB, LANES), jnp.float32),
        in_specs=[vmem()] * 4,
        out_specs=vmem(),
        compiler_params=small(),
        name="render",
    )(recv, maps_hi, maps_lo, entry_own)
    turned = lax.all_to_all(image, "depth", split_axis=0, concat_axis=0, tiled=True, axis_index_groups=[turn])
    return pl.pallas_call(
        functools.partial(unpack_kernel, per, turn),
        out_shape=jax.ShapeDtypeStruct((1, 3, rows // depth, lateral), jnp.float32),
        in_specs=[vmem()],
        out_specs=vmem(),
        compiler_params=small(),
        name="unpack",
    )(turned)


def with_arrays(volume, step_weights, row_interp, col_interp, tf_table, materials, entry):
    all_steps = lax.all_gather(step_weights, "view", axis=0, tiled=True)
    all_cols = lax.all_gather(col_interp, "view", axis=0, tiled=True)
    views, steps, edge = all_steps.shape
    depth = lax.axis_size("depth")
    planes, lateral, _ = volume.shape
    devices = views * depth
    per = lateral // depth
    rows = devices * planes
    tiles_z, tiles_y = materials.shape[:2]
    step_length = 2.0 / (steps * depth)
    cells = volume.reshape(planes, tiles_y, edge, depth, edge)
    first = jnp.einsum("pujbi,vsi->vpujbs", cells, all_steps, precision=HIGHEST)
    second = jnp.einsum("vpujbs,vcj->vpucbs", first, all_cols, precision=HIGHEST)
    second = second.reshape(views, planes, depth, per, depth, steps).transpose(0, 2, 1, 3, 4, 5)
    second = second.reshape(devices, planes * per * depth * steps)
    own = tf_table[materials[:, :, 0]].transpose(1, 0, 2).reshape(tiles_y, tiles_z * COEF)
    own = jnp.tile(jnp.repeat(own, edge // per, axis=0), (views, 1))
    payload = jnp.concatenate([second, own], axis=1)
    payload = jnp.pad(payload, ((0, 0), (0, -payload.shape[1] % LANES)))
    payload = payload.reshape(devices, -1, 1, LANES)
    recv = lax.all_to_all(payload, ("view", "depth"), split_axis=0, concat_axis=0, tiled=True)
    recv = recv.reshape(devices, -1)
    size = second.shape[1]
    coef = recv[:depth, size : size + tiles_z * COEF].reshape(depth, tiles_z, COEF)
    coef = jnp.repeat(coef.transpose(2, 1, 0), edge, axis=1)[:, :, None, :, None]
    third = recv[:, :size].reshape(tiles_z, edge, per, depth, steps)
    third = jnp.einsum("tkcbs,rk->trcbs", third, row_interp[0], precision=HIGHEST)
    samples = third.reshape(rows, per, depth, steps)
    entry_own = lax.dynamic_slice_in_dim(entry[0], lax.axis_index("depth") * per, per, 1)
    live = (entry_own[:, :, None] <= jnp.arange(depth)).astype(jnp.float32)
    tau = step_length * live[..., None] * jax.nn.softplus(coef[6] * samples + coef[7])
    flat = tau.reshape(rows, per, depth * steps)
    earlier = (jnp.cumsum(flat, axis=2) - flat).reshape(tau.shape)
    weights = jnp.exp(-earlier) * (1.0 - jnp.exp(-tau))
    emission = jax.nn.softplus(coef[0:3] * samples + coef[3:6])
    image = jnp.sum(weights * emission, axis=(3, 4))
    turned = lax.all_to_all(image, "depth", split_axis=1, concat_axis=2, tiled=True)
    return turned[None]


def shards(volume, step_weights, row_interp, col_interp, tf_table, materials, entry):
    views = lax.axis_size("view")
    depth = lax.axis_size("depth")
    planes, lateral, span = volume.shape
    steps, edge = step_weights.shape[1:]
    rows = views * depth * planes
    fits = (
        depth == SUB
        and steps == SUB
        and edge == LANES // 2
        and lateral == LANES
        and rows == LANES
        and views in (2, 4, 8)
        and span == depth * edge
    )
    run = with_kernels if fits else with_arrays
    return run(volume, step_weights, row_interp, col_interp, tf_table, materials, entry)


def solution(mesh):
    placed = (
        P(("view", "depth"), None, None),
        P("view", None, None),
        P("view", None, None),
        P("view", None, None),
        P(),
        P(None, None, "depth"),
        P("view", None, None),
    )
    return jax.shard_map(
        shards,
        mesh=mesh,
        in_specs=placed,
        out_specs=P("view", None, "depth", None),
        check_vma=False,
    )
```

profile of v0, /device:TPU:0, one launch (start us, length us, event | category | flops | bytes accessed | tf_op | source)
XLA Modules:
  0.0 39.9 jit_solution(785043113359317327)
XLA Ops:
  0.0 0.8 %pack.1.refs_0_ = f32[1,40,128]{2,1,0:T(8,128)S(1)} custom-call(f32[1,8,64]{2,1,0:T(8,128)} %steps_hbm.1, f32[1,64,64]{2,1,0:T(8,128)} %cols_hbm.1), custom_call_target="tpu_custom_call" | custom-call | tf_op jit(solution)/shard_map/pack/pallas_call | solution.py:269
  0.9 0.6 %collective-permute-start.2 = (f32[1,40,128]{2,1,0:T(8,128)S(1)}, f32[1,40,128]{2,1,0:T(8,128)S(1)}, u32[]{:S(2)}, u32[]{:S(2)}) collective-permute-start(f32[1,40,128]{2,1,0:T(8,128)S(1)} %pack.1.refs_0_), channel_id=1, source_target_pairs={{0,8},{8,0},{16,24},{24,16},{1,9},{9,1},{17,25},{25,17},{2,10},{10... | collective-permute-start | bytes 61448 | tf_op jit(solution)/shard_map/ppermute | solution.py:284
  1.4 2.6 %collective-permute-start.1 = (f32[1,40,128]{2,1,0:T(8,128)S(1)}, f32[1,40,128]{2,1,0:T(8,128)S(1)}, u32[]{:S(2)}, u32[]{:S(2)}) collective-permute-start(f32[1,40,128]{2,1,0:T(8,128)S(1)} %pack.1.refs_0_), channel_id=1, source_target_pairs={{0,24},{8,16},{16,8},{24,0},{1,25},{9,17},{17,9},{25,1},{2,26},{10... | collective-permute-start | bytes 61448 | tf_op jit(solution)/shard_map/ppermute | solution.py:284
  4.0 0.0 collective-permute-start
  4.0 1.6 %prepare.1 = (bf16[512,512]{1,0:T(8,128)(2,1)S(1)}, bf16[512,512]{1,0:T(8,128)(2,1)S(1)}, bf16[128,128]{1,0:T(8,128)(2,1)S(1)}, bf16[128,128]{1,0:T(8,128)(2,1)S...) custom-call(s32[1]{0:T(128)} %bitcast.1.depth_ref, s32[2,1,2]{2,1,0:T(1,128)} %bitcast.9, f32[8,8]{1,0:T(8,128)} %table_hbm.1, ...), custom_call_target="tpu_custom_call" | custom-call | flops 2000000000 | bytes 4000000 | tf_op jit(solution)/shard_map/prepare/pallas_call | solution.py:285
  5.7 0.0 collective-permute-done.2.refs_1_
  5.7 0.8 %shard_map.73.refs_2_ = f32[1056,128]{1,0:T(8,128)S(1)} custom-call(s32[1]{0:T(128)} %bitcast.view_ref, bf16[512,512]{1,0:T(8,128)(2,1)S(1)} %get-tuple-element.11.hi_ref, bf16[512,512]{1,0:T(8,128)(2,1)S(1)} %get-tuple-element.12.lo_ref, f32[2,128]{1,0:T(2,128)S(1)} %get-tuple-element.13.coef_ref, f32[1,40,128]{2,1,0:T(8,128)S(1)} %pack.1.refs_0_, ...), custom_call_target="tpu_custom_call" | custom-call | flops 1000000000 | bytes 2000000 | tf_op jit(solution)/shard_map/pallas_call | solution.py:315
  6.5 0.0 collective-permute-done.1.refs_1_
  6.5 1.3 %collective-permute-done.refs_0_ = f32[1,40,128]{2,1,0:T(8,128)S(1)} collective-permute-done((f32[1,40,128]{2,1,0:T(8,128)S(1)}, f32[1,40,128]{2,1,0:T(8,128)S(1)}, u32[]{:S(2)}, u32[]{:S(2)}) %collective-permute-start) | collective-permute-done | bytes 20512 | tf_op jit(solution)/shard_map/ppermute | solution.py:284
  7.8 0.8 %shard_map.74 = f32[1056,128]{1,0:T(8,128)S(1)} custom-call(s32[1]{0:T(128)} %bitcast.view_ref, bf16[512,512]{1,0:T(8,128)(2,1)S(1)} %get-tuple-element.11.hi_ref, bf16[512,512]{1,0:T(8,128)(2,1)S(1)} %get-tuple-element.12.lo_ref, f32[2,128]{1,0:T(2,128)S(1)} %get-tuple-element.13.coef_ref, ...), custom_call_target="tpu_custom_call", output_to_operand_aliasing={{}: (6, {})} | custom-call | flops 1000000000 | bytes 2000000 | tf_op jit(solution)/shard_map/pallas_call | solution.py:315
  8.6 19.4 %all_to_all.10 = f32[32,33,1,128]{3,2,1,0:T(1,128)S(1)} all-to-all(f32[32,33,1,128]{3,2,1,0:T(1,128)S(1)} %bitcast.8), channel_id=1, replica_groups={{0,2,4,6,8,10,12,14,16,18,20,22,24,26,28,30,1,3,5,7,9,11,13,15,17,19,21..., dimensions={0} | all-to-all | bytes 1081344 | tf_op jit(solution)/shard_map/all_to_all | solution.py:327
  28.0 1.7 %render.1 = f32[8,8,128]{2,1,0:T(8,128)S(1)} custom-call(f32[1056,128]{1,0:T(8,128)S(1)} %bitcast.7, bf16[128,128]{1,0:T(8,128)(2,1)S(1)} %get-tuple-element.14.maps_hi_ref, bf16[128,128]{1,0:T(8,128)(2,1)S(1)} %get-tuple-element.15.maps_lo_ref, s32[16,128]{1,0:T(8,128)S(1)} %get-tuple-element.16.entry_ref), custom_call_target="tpu_custom_call" | custom-call | tf_op jit(solution)/shard_map/render/pallas_call | solution.py:329
  29.7 9.4 %all_to_all.11.recv_ref = f32[8,8,128]{2,1,0:T(8,128)S(1)} all-to-all(f32[8,8,128]{2,1,0:T(8,128)S(1)} %render.1), channel_id=1, replica_groups={{5,6,7,0,1,2,3,4},{13,14,15,8,9,10,11,12},{21,22,23,16,17,18,19,20},{29..., dimensions={0} | all-to-all | bytes 65536 | tf_op jit(solution)/shard_map/all_to_all | solution.py:337
  39.2 0.7 %unpack.1 = f32[1,3,16,128]{3,2,1,0:T(8,128)} custom-call(f32[8,8,128]{2,1,0:T(8,128)S(1)} %all_to_all.11.recv_ref), custom_call_target="tpu_custom_call" | custom-call | tf_op jit(solution)/shard_map/unpack/pallas_call | solution.py:338
Async XLA Ops:
  0.9 4.8 %collective-permute-start.2 = (f32[1,40,128]{2,1,0:T(8,128)S(1)}, f32[1,40,128]{2,1,0:T(8,128)S(1)}, u32[]{:S(2)}, u32[]{:S(2)}) collective-permute-start(f32[1,40,128]{2,1,0:T(8,128)S(1)} %pack.1.refs_0_), channel_id=1, source_target_pairs={{0,8},{8,0},{16,24},{24,16},{1,9},{9,1},{17,25},{25,17},{2,10},{10... | collective-permute-start | bytes 61448 | tf_op jit(solution)/shard_map/ppermute | solution.py:284
  1.4 5.0 %collective-permute-start.1 = (f32[1,40,128]{2,1,0:T(8,128)S(1)}, f32[1,40,128]{2,1,0:T(8,128)S(1)}, u32[]{:S(2)}, u32[]{:S(2)}) collective-permute-start(f32[1,40,128]{2,1,0:T(8,128)S(1)} %pack.1.refs_0_), channel_id=1, source_target_pairs={{0,24},{8,16},{16,8},{24,0},{1,25},{9,17},{17,9},{25,1},{2,26},{10... | collective-permute-start | bytes 61448 | tf_op jit(solution)/shard_map/ppermute | solution.py:284
  4.0 3.8 %collective-permute-start = (f32[1,40,128]{2,1,0:T(8,128)S(1)}, f32[1,40,128]{2,1,0:T(8,128)S(1)}, u32[]{:S(2)}, u32[]{:S(2)}) collective-permute-start(f32[1,40,128]{2,1,0:T(8,128)S(1)} %pack.1.refs_0_), channel_id=1, source_target_pairs={{0,16},{8,24},{16,0},{24,8},{1,17},{9,25},{17,1},{25,9},{2,18},{10... | collective-permute-start | bytes 61448 | tf_op jit(solution)/shard_map/ppermute | solution.py:284
where the time goes:
time: 40.1 us; the launch traced here: 39.9 us
  blocking collectives  28.8 us (72%)
  Pallas kernels  6.47 us (16%)
  starting transfers between devices  3.19 us (8%)
  waiting for transfers between devices  1.33 us (3%)
    all_to_all x1, blocking collectives, with_kernels(): lax.all_to_all(blocks, ('view', 'depth'), split_axis=0, concat_axis=0, ti...  19.4 us
    all_to_all x1, blocking collectives, with_kernels(): lax.all_to_all(image, 'depth', split_axis=0, concat_axis=0, tiled=True, a...  9.44 us
    ppermute x3, starting transfers between devices, with_kernels(): maps.append(lax.ppermute(own, 'view', [(i, i ^ k) for i in range(views)]))  3.19 us
    pallas_call x1, Pallas kernels, with_kernels(): pl.pallas_call(functools.partial(render_kernel, step_length, planes, orde...  1.75 us
    pallas_call x1, Pallas kernels, with_kernels(): pl.pallas_call(functools.partial(prepare_kernel, order), out_shape=[jax.S...  1.59 us
    pallas_call x2, Pallas kernels, with_kernels(): pl.pallas_call(functools.partial(send_kernel, order, depth, planes, pair)...  1.56 us
    ppermute x3, waiting for transfers between devices, with_kernels(): maps.append(lax.ppermute(own, 'view', [(i, i ^ k) for i in range(views)]))  1.33 us
    pallas_call x1, Pallas kernels, with_kernels(): pl.pallas_call(pack_kernel, out_shape=jax.ShapeDtypeStruct((1, edge // 2...  0.85 us
  transfers between devices with their start and end apart: 3, of which 1 were waited for; matrix products, arithmetic and copies ran while one was open for 0% of the time, Pallas kernels for 6%

commit v1 on v0

--- a/solution.py
+++ b/solution.py
@@ -11,6 +11,7 @@
 LANES = 128
 SUB = 8
 COEF = 8
+CORES = 2
 HIGHEST = lax.Precision.HIGHEST
 NT = (((1,), (1,)), ((), ()))
 NN = (((1,), (0,)), ((), ()))
@@ -27,146 +28,141 @@
     return jnp.maximum(v, 0.0) + jnp.where(e < 1e-4, small, jnp.log(1.0 + e))
 
 
-def pack_kernel(steps_hbm, cols_hbm, out_ref, steps_ref, cols_ref, sems):
-    copies = [
-        pltpu.make_async_copy(cols_hbm, cols_ref, sems.at[0]),
-        pltpu.make_async_copy(steps_hbm, steps_ref, sems.at[1]),
+def fetch_kernel(
+    steps_hbm, cols_hbm, classes_hbm, table_hbm, vol_hbm, row_hbm, entry_hbm,
+    packed_ref, vol_ref, row_ref, entry_ref, coef_ref,
+    steps_ref, cols_ref, classes_ref, table_ref, sems,
+):
+    pieces = [
+        (cols_hbm, cols_ref), (steps_hbm, steps_ref), (classes_hbm, classes_ref), (table_hbm, table_ref),
+        (row_hbm, row_ref), (entry_hbm, entry_ref),
     ]
-    for copy in copies:
-        copy.start()
-    for copy in copies:
-        copy.wait()
-    edge = cols_ref.shape[1]
-    out_ref[0, : edge // 2] = jnp.concatenate([cols_ref[0, : edge // 2], cols_ref[0, edge // 2 :]], axis=1)
-    out_ref[0, edge // 2 :] = jnp.concatenate([steps_ref[0], steps_ref[0]], axis=1)
-
-
-def prepare_kernel(
-    order, depth_ref, classes_hbm, table_hbm, vol_hbm, row_hbm, entry_hbm,
-    hi_ref, lo_ref, maps_hi_ref, maps_lo_ref, entry_own_ref, coef_ref,
-    classes_ref, table_ref, vol_ref, row_ref, entry_ref, turned_ref, moved_ref, sems,
-):
-    planes, lateral, _ = vol_ref.shape
-    tiles_z, tiles_y = classes_ref.shape[0], classes_ref.shape[2]
-    per = entry_own_ref.shape[0]
-    pieces = [(vol_hbm.at[p], vol_ref.at[p]) for p in range(planes)]
-    pieces += [(entry_hbm, entry_ref), (row_hbm, row_ref), (classes_hbm, classes_ref), (table_hbm, table_ref)]
+    pieces += [(vol_hbm.at[p], vol_ref.at[p]) for p in range(vol_ref.shape[0])]
     copies = [pltpu.make_async_copy(*piece, sems.at[n]) for n, piece in enumerate(pieces)]
     for copy in copies:
         copy.start()
-    for copy in copies[planes:]:
+    for copy in copies[:4]:
         copy.wait()
+    edge = cols_ref.shape[1]
+    packed_ref[0, : edge // 2] = jnp.concatenate([cols_ref[0, : edge // 2], cols_ref[0, edge // 2 :]], axis=1)
+    packed_ref[0, edge // 2 :] = jnp.concatenate([steps_ref[0], steps_ref[0]], axis=1)
     lane = lax.broadcasted_iota(jnp.int32, (1, LANES), 1)
-    for u in range(tiles_y):
+    for u in range(classes_ref.shape[2]):
         row = jnp.zeros((1, LANES), jnp.float32)
-        for t in range(tiles_z):
+        for t in range(classes_ref.shape[0]):
             for ch in range(COEF):
                 row = jnp.where(lane == t * COEF + ch, table_ref[classes_ref[t, 0, u], ch], row)
         coef_ref[u : u + 1] = row
+    for copy in copies[4:]:
+        copy.wait()
+
+
+def prepare_kernel(
+    order, planes, view_ref, depth_ref, vol_ref, row_ref, entry_ref,
+    hi_ref, lo_ref, maps_hi_ref, maps_lo_ref, entry_own_ref,
+    turned_ref, moved_ref,
+):
+    per = entry_own_ref.shape[0]
     turned = row_ref[0].T
     zero = jnp.zeros_like(turned)
-    maps = jnp.concatenate(
+    tiles_z = turned_ref.shape[0] // turned.shape[0]
+    turned_ref[...] = jnp.concatenate(
         [jnp.concatenate([turned if i == t else zero for i in range(tiles_z)], axis=1) for t in range(tiles_z)],
         axis=0,
     )
-    turned_ref[...] = maps
-    for p in range(planes):
-        for n, device in enumerate(order):
-            to, at = p * len(order) + n, device * planes + p
-            moved_ref[to : to + 1] = turned_ref[at : at + 1]
+    core = view_ref[0] % CORES
+    depth = entry_ref.shape[2] // per
+    for swapped in range(CORES):
+        slab = (core ^ swapped) * depth * planes
+        for p in range(planes):
+            for n, (chip, d) in enumerate(order):
+                to = (swapped * planes + p) * len(order) + n
+                at = slab + (chip * CORES * depth + d) * planes + p
+                moved_ref[to : to + 1] = turned_ref[pl.ds(at, 1), :]
     maps_hi_ref[...], maps_lo_ref[...] = split(moved_ref[...])
     turned = entry_ref[0].astype(jnp.float32).T
     own = jnp.zeros((per, turned.shape[1]), jnp.float32)
-    for d in range(turned.shape[0] // per):
+    for d in range(depth):
         own = jnp.where(depth_ref[0] == d, turned[d * per : (d + 1) * per], own)
     entry_own_ref[...] = own.astype(jnp.int32)
-    for p in range(planes):
-        copies[p].wait()
+    halve_kernel(vol_ref, hi_ref, lo_ref)
+
+
+def halve_kernel(vol_ref, hi_ref, lo_ref):
+    lateral = vol_ref.shape[1]
+    for p in range(vol_ref.shape[0]):
         at = slice(p * lateral, (p + 1) * lateral)
         hi_ref[at], lo_ref[at] = split(vol_ref[p])
 
 
-def send_kernel(order, depth, planes, pair, view_ref, hi_ref, lo_ref, coef_ref, *refs):
+def send_kernel(order, depth, planes, flip, view_ref, hi_ref, lo_ref, hi_swapped_ref, lo_swapped_ref, coef_ref, map_ref, *refs):
     out_ref = refs[-1]
-    map_refs = refs[:2]
-    edge = map_refs[0].shape[2] // 2
+    edge = map_ref.shape[2] // 2
     lateral, span = hi_ref.shape[0] // planes, hi_ref.shape[1]
     bricks = span // edge
     per = lateral // depth
-    block_rows = planes * SUB + 1
-    views = len(order) // depth
-    view = [view_ref[0] ^ (2 * pair + k) for k in range(2)]
-
-    def first_row(k, d):
-        row = order.index(d) * block_rows
-        for v in range(1, views):
-            row = jnp.where(view[k] == v, order.index(v * depth + d) * block_rows, row)
-        return row
-
-    starts = [[first_row(k, d) for d in range(depth)] for k in range(2)]
-
-    weights = jnp.concatenate([ref[0, edge // 2 :] for ref in map_refs], axis=0)
+    block_rows = CORES * planes * SUB + 1
+    chip = (view_ref[0] // CORES) ^ flip
+    starts = []
+    for d in range(depth):
+        row = order.index((0, d)) * block_rows
+        for x in range(1, len(order) // depth):
+            row = jnp.where(chip == x, order.index((x, d)) * block_rows, row)
+        starts.append(row)
+
+    weights = map_ref[0, edge // 2 :]
     tiled = jnp.concatenate([weights] * (span // LANES), axis=1)
     lane = lax.broadcasted_iota(jnp.int32, (bricks, span), 1)
     brick = lax.broadcasted_iota(jnp.int32, (bricks, span), 0)
     own = lane // edge == brick
     ray = jnp.where(own[None], tiled[:, None, :], 0.0).reshape(weights.shape[0] * bricks, span)
     ray_hi, ray_lo = split(ray)
-    both = lax.dot_general(
-        hi_ref[...], jnp.concatenate([ray_hi, ray_lo], axis=0), NT, preferred_element_type=jnp.float32
-    )
-    first = both[:, :LANES] + (
-        both[:, LANES:] + lax.dot_general(lo_ref[...], ray_hi, NT, preferred_element_type=jnp.float32)
-    )
-    first_hi, first_lo = split(first)
+    ray_hi = jnp.concatenate([ray_hi, ray_hi], axis=0)
+    ray_both = jnp.concatenate([ray_hi, ray_lo, ray_lo], axis=0)
 
     half = lax.broadcasted_iota(jnp.int32, (SUB, LANES), 1) < edge
     left = lax.broadcasted_iota(jnp.int32, (edge // 2, LANES), 1) < edge
-    rows = []
-    for ref in map_refs:
-        c = ref[0, : edge // 2]
-        turned = pltpu.roll(c, edge, 1)
-        rows += [jnp.where(left, c, 0.0), jnp.where(left, turned, 0.0)]
-        rows += [jnp.where(left, 0.0, turned), jnp.where(left, 0.0, c)]
+    c = map_ref[0, : edge // 2]
+    turned = pltpu.roll(c, edge, 1)
+    rows = [jnp.where(left, c, 0.0), jnp.where(left, turned, 0.0)]
+    rows += [jnp.where(left, 0.0, turned), jnp.where(left, 0.0, c)]
     maps_hi, maps_lo = split(jnp.concatenate(rows, axis=0))
     maps = jnp.concatenate([maps_hi, maps_lo], axis=1)
-    for couple in range(planes // 2):
-        at = [slice((2 * couple + i) * lateral, (2 * couple + i + 1) * lateral) for i in range(2)]
-        high = jnp.concatenate([first_hi[i] for i in at], axis=1)
-        low = jnp.concatenate([first_lo[i] for i in at], axis=1)
-        second = lax.dot_general(
-            maps, jnp.concatenate([high, high], axis=0), NN, preferred_element_type=jnp.float32
-        ) + lax.dot_general(maps_hi, low, NN, preferred_element_type=jnp.float32)
-        for i in range(2):
-            plane = 2 * couple + i
-            for k in range(2):
+    for swapped, (high_ref, low_ref) in enumerate(((hi_ref, lo_ref), (hi_swapped_ref, lo_swapped_ref))):
+        both = lax.dot_general(high_ref[...], ray_both, NT, preferred_element_type=jnp.float32)
+        first = both[:, :LANES] + (
+            both[:, LANES:] + lax.dot_general(low_ref[...], ray_hi, NT, preferred_element_type=jnp.float32)
+        )
+        first_hi, first_lo = split(first)
+        for couple in range(planes // 2):
+            at = [slice((2 * couple + i) * lateral, (2 * couple + i + 1) * lateral) for i in range(2)]
+            high = jnp.concatenate([first_hi[i] for i in at], axis=1)
+            low = jnp.concatenate([first_lo[i] for i in at], axis=1)
+            second = lax.dot_general(
+                maps, jnp.concatenate([high, high], axis=0), NN, preferred_element_type=jnp.float32
+            ) + lax.dot_general(maps_hi, low, NN, preferred_element_type=jnp.float32)
+            for i in range(2):
+                plane = swapped * planes + 2 * couple + i
                 for d in range(depth):
-                    base = k * lateral + d * per
+                    base = d * per
                     a = second[base : base + SUB, i * LANES : (i + 1) * LANES]
                     b = second[base + SUB : base + 2 * SUB, i * LANES : (i + 1) * LANES]
-                    if k == 0:
-                        b = pltpu.roll(b, edge, 1)
-                    else:
-                        a = pltpu.roll(a, edge, 1)
-                    at_row = starts[k][d] + plane * SUB
-                    out_ref[pl.ds(at_row, SUB), :] = jnp.where(half, a, b)
-    for k in range(2):
-        for d in range(depth):
-            u = d * per // edge
-            at_row = starts[k][d] + block_rows - 1
-            out_ref[pl.ds(at_row, 1), :] = coef_ref[u : u + 1]
+                    out_ref[pl.ds(starts[d] + plane * SUB, SUB), :] = jnp.where(half, a, b)
+    for d in range(depth):
+        u = d * per // edge
+        out_ref[pl.ds(starts[d] + block_rows - 1, 1), :] = coef_ref[u : u + 1]
 
 
 def render_kernel(step_length, planes, order, turn, recv_ref, maps_hi_ref, maps_lo_ref, entry_ref, out_ref):
     block_rows = planes * SUB + 1
-    sources = recv_ref.shape[0] // block_rows
+    sources = len(order)
     columns, rows = entry_ref.shape
     bricks = steps = SUB
     maps_hi = maps_hi_ref[...]
     maps = jnp.concatenate([maps_hi, maps_hi], axis=0)
     maps_lo = maps_lo_ref[...]
 
-    ends = [(order.index(b) + 1) * block_rows for b in range(bricks)]
+    ends = [(order.index((0, b)) + 1) * block_rows for b in range(bricks)]
     packed = jnp.concatenate([recv_ref[end - 1 : end] for end in ends], axis=0)
     lane = lax.broadcasted_iota(jnp.int32, (bricks, rows), 1)
     upper = lane >= rows // 2
@@ -232,9 +228,11 @@
 
 
 def orders(views, depth):
-    order = [v * depth + z * 2 + y for y in range(2) for v in range(views) for z in range(depth // 2)]
-    first = depth // 2 + 1
-    return order, list(range(first, depth)) + list(range(first))
+    chips = views // CORES
+    order = [(x, z * 2 + y) for y in range(2) for x in range(chips) for z in range(depth // 2)]
+    first = order.index((chips - 1, depth // 2 + 1))
+    turn = depth // 2 + 1
+    return order[first:] + order[:first], list(range(turn, depth)) + list(range(turn))
 
 
 def vmem():
@@ -263,71 +261,77 @@
     rows = devices * planes
     step_length = 2.0 / (steps * depth)
     tiles_y = lateral // edge
-    block_rows = planes * SUB + 1
+    block_rows = CORES * planes * SUB + 1
     order, turn = orders(views, depth)
+    groups = [[(x * CORES + core) * depth + d for x, d in order] for core in range(CORES)]
     depth_at = lax.axis_index("depth").reshape(1)
-    own = pl.pallas_call(
-        pack_kernel,
-        out_shape=jax.ShapeDtypeStruct((1, edge // 2 + steps, 2 * edge), jnp.float32),
-        in_specs=[hbm()] * 2,
-        out_specs=vmem(),
+    view_at = lax.axis_index("view").reshape(1)
+    slab = lax.ppermute(volume, "view", [(i, i ^ 1) for i in range(views)])
+    own, vol, row, entry_all, coef = pl.pallas_call(
+        fetch_kernel,
+        out_shape=[
+            jax.ShapeDtypeStruct((1, edge // 2 + steps, 2 * edge), jnp.float32),
+            jax.ShapeDtypeStruct(volume.shape, volume.dtype),
+            jax.ShapeDtypeStruct(row_interp.shape, row_interp.dtype),
+            jax.ShapeDtypeStruct(entry.shape, entry.dtype),
+            jax.ShapeDtypeStruct((tiles_y, LANES), jnp.float32),
+        ],
+        in_specs=[hbm()] * 7,
+        out_specs=[vmem()] * 5,
         scratch_shapes=[
             pltpu.VMEM(step_weights.shape, jnp.float32),
             pltpu.VMEM(col_interp.shape, jnp.float32),
-            pltpu.SemaphoreType.DMA((2,)),
+            pltpu.SMEM((materials.shape[0], 1, tiles_y), jnp.int32),
+            pltpu.SMEM(tf_table.shape, jnp.float32),
+            pltpu.SemaphoreType.DMA((planes + 6,)),
         ],
         compiler_params=small(),
-        name="pack",
-    )(in_hbm(step_weights), in_hbm(col_interp))
-    maps = [own]
-    for k in range(1, views):
-        maps.append(lax.ppermute(own, "view", [(i, i ^ k) for i in range(views)]))
-    hi, lo, maps_hi, maps_lo, entry_own, coef = pl.pallas_call(
-        functools.partial(prepare_kernel, order),
+        name="fetch",
+    )(*map(in_hbm, (step_weights, col_interp, materials.transpose(0, 2, 1), tf_table, volume, row_interp, entry)))
+    far = lax.ppermute(own, "view", [(i, i ^ CORES) for i in range(views)])
+    hi, lo, maps_hi, maps_lo, entry_own = pl.pallas_call(
+        functools.partial(prepare_kernel, order, planes),
         out_shape=[
             jax.ShapeDtypeStruct((planes * lateral, span), jnp.bfloat16),
             jax.ShapeDtypeStruct((planes * lateral, span), jnp.bfloat16),
             jax.ShapeDtypeStruct((rows, rows), jnp.bfloat16),
             jax.ShapeDtypeStruct((rows, rows), jnp.bfloat16),
             jax.ShapeDtypeStruct((per, rows), jnp.int32),
-            jax.ShapeDtypeStruct((tiles_y, LANES), jnp.float32),
         ],
-        in_specs=[smem()] + [hbm()] * 5,
-        out_specs=[vmem()] * 6,
-        scratch_shapes=[
-            pltpu.SMEM((materials.shape[0], 1, tiles_y), jnp.int32),
-            pltpu.SMEM(tf_table.shape, jnp.float32),
-            pltpu.VMEM(volume.shape, jnp.float32),
-            pltpu.VMEM(row_interp.shape, jnp.float32),
-            pltpu.VMEM(entry.shape, jnp.int32),
-            pltpu.VMEM((rows, rows), jnp.float32),
-            pltpu.VMEM((rows, rows), jnp.float32),
-            pltpu.SemaphoreType.DMA((planes + 4,)),
-        ],
+        in_specs=[smem()] * 2 + [vmem()] * 3,
+        out_specs=[vmem()] * 5,
+        scratch_shapes=[pltpu.VMEM((rows, rows), jnp.float32), pltpu.VMEM((rows, rows), jnp.float32)],
         compiler_params=small(),
         cost_estimate=pl.CostEstimate(flops=2_000_000_000, bytes_accessed=4_000_000, transcendentals=0),
         name="prepare",
-    )(depth_at, *map(in_hbm, (materials.transpose(0, 2, 1), tf_table, volume, row_interp, entry)))
-    view_at = lax.axis_index("view").reshape(1)
+    )(view_at, depth_at, vol, row, entry_all)
+    hi_swapped, lo_swapped = pl.pallas_call(
+        halve_kernel,
+        out_shape=[jax.ShapeDtypeStruct((planes * lateral, span), jnp.bfloat16)] * 2,
+        in_specs=[vmem()],
+        out_specs=[vmem()] * 2,
+        compiler_params=small(),
+        name="halve",
+    )(slab)
     blocks = []
-    for pair in range(views // 2):
+    for flip, packed in enumerate((own, far)):
         blocks = [
             pl.pallas_call(
-                functools.partial(send_kernel, order, depth, planes, pair),
-                out_shape=jax.ShapeDtypeStruct((devices * block_rows, LANES), jnp.float32),
-                in_specs=[smem()] + [vmem()] * (5 + len(blocks)),
+                functools.partial(send_kernel, order, depth, planes, flip),
+                out_shape=jax.ShapeDtypeStruct((len(order) * block_rows, LANES), jnp.float32),
+                in_specs=[smem()] + [vmem()] * (6 + len(blocks)),
                 out_specs=vmem(),
-                input_output_aliases={6: 0} if blocks else {},
+                input_output_aliases={7: 0} if blocks else {},
                 compiler_params=small(),
                 cost_estimate=pl.CostEstimate(flops=1_000_000_000, bytes_accessed=2_000_000, transcendentals=0),
-            )(view_at, hi, lo, coef, *maps[2 * pair : 2 * pair + 2], *blocks)
+            )(view_at, hi, lo, hi_swapped, lo_swapped, coef, packed, *blocks)
         ]
     blocks = blocks[0]
-    blocks = blocks.reshape(devices, block_rows, 1, LANES)
-    recv = lax.all_to_all(blocks, ("view", "depth"), split_axis=0, concat_axis=0, tiled=True, axis_index_groups=[order])
-    recv = recv.reshape(devices * block_rows, LANES)
+    blocks = blocks.reshape(len(order), block_rows, 1, LANES)
+    recv = lax.all_to_all(blocks, ("view", "depth"), split_axis=0, concat_axis=0, tiled=True, axis_index_groups=groups)
+    recv = recv.reshape(len(order) * block_rows, LANES)
     image = pl.pallas_call(
-        functools.partial(render_kernel, step_length, planes, order, turn),
+        functools.partial(render_kernel, step_length, CORES * planes, order, turn),
         out_shape=jax.ShapeDtypeStruct((depth, SUB, LANES), jnp.float32),
         in_specs=[vmem()] * 4,
         out_specs=vmem(),
@@ -398,7 +402,7 @@
         and edge == LANES // 2
         and lateral == LANES
         and rows == LANES
-        and views in (2, 4, 8)
+        and views == 2 * CORES
         and span == depth * edge
     )
     run = with_kernels if fits else with_arrays

time: 40.1 us -> 38.1 us (0.950)
  waiting for transfers between devices: 1.33 us -> 0.11 us
  blocking collectives: 28.8 us -> 28.1 us
    ppermute x3 -> x2, waiting for transfers between devices: 1.33 us -> 0.11 us  [the longest x1 0.11 us: with_kernels(): far = lax.ppermute(own, 'view', [(i, i ^ CORES) for i in range(views)])]
    all_to_all x1, blocking collectives: 9.44 us -> 8.43 us  [with_kernels(): lax.all_to_all(image, 'depth', split_axis=0, concat_axis=0, tiled=True, a...]
    ppermute x3 -> x2, starting transfers between devices: 3.19 us -> 3.04 us  [the longest x1 2.54 us: with_kernels(): far = lax.ppermute(own, 'view', [(i, i ^ CORES) for i in range(views)])]
    pallas_call x5 -> x6, Pallas kernels: 5.75 us -> 5.89 us  [the longest x2 2.24 us: with_kernels(): pl.pallas_call(functools.partial(send_kernel, order, depth, planes, flip)...]
  transfers between devices with their start and end apart: 3 -> 2, of which waited for: 1 -> 1; matrix products, arithmetic and copies ran while one was open for 0% -> 0% of each run, Pallas kernels for 6% -> 8%
where the time goes in v1:
time: 38.1 us; the launch traced here: 37.9 us
  blocking collectives  28.1 us (74%)
  Pallas kernels  6.61 us (17%)
  starting transfers between devices  3.04 us (8%)
    all_to_all x1, blocking collectives, with_kernels(): lax.all_to_all(blocks, ('view', 'depth'), split_axis=0, concat_axis=0, ti...  19.7 us
    all_to_all x1, blocking collectives, with_kernels(): lax.all_to_all(image, 'depth', split_axis=0, concat_axis=0, tiled=True, a...  8.43 us
    ppermute x1, starting transfers between devices, with_kernels(): far = lax.ppermute(own, 'view', [(i, i ^ CORES) for i in range(views)])  2.54 us
    pallas_call x2, Pallas kernels, with_kernels(): pl.pallas_call(functools.partial(send_kernel, order, depth, planes, flip)...  2.24 us
    pallas_call x1, Pallas kernels, with_kernels(): pl.pallas_call(functools.partial(render_kernel, step_length, CORES * plan...  1.75 us
    pallas_call x1, Pallas kernels, with_kernels(): pl.pallas_call(fetch_kernel, out_shape=[jax.ShapeDtypeStruct((1, edge //...  1.36 us
  transfers between devices with their start and end apart: 2, of which 1 were waited for; matrix products, arithmetic and copies ran while one was open for 0% of the time, Pallas kernels for 8%

profile of v1, /device:TPU:0, one launch (start us, length us, event | category | flops | bytes accessed | tf_op | source)
XLA Modules:
  0.0 37.9 jit_solution(529217417695612103)
XLA Ops:
  0.0 0.5 %collective-permute-start = (f32[4,128,512]{2,1,0:T(8,128)}, f32[4,128,512]{2,1,0:T(8,128)S(1)}, u32[]{:S(2)}, u32[]{:S(2)}) collective-permute-start(f32[4,128,512]{2,1,0:T(8,128)} %vol_hbm.1), channel_id=1, source_target_pairs={{0,8},{8,0},{16,24},{24,16},{1,9},{9,1},{17,25},{25,17},{2,10},{10... | collective-permute-start | bytes 3145736 | tf_op jit(solution)/shard_map/ppermute | solution.py:269
  0.5 1.4 %fetch.1 = (f32[1,40,128]{2,1,0:T(8,128)S(1)}, f32[4,128,512]{2,1,0:T(8,128)S(1)}, f32[1,64,64]{2,1,0:T(8,128)S(1)}, s32[1,128,128]{2,1,0:T(8,128)S(1)}, f32[2,128]{1,0:T(2,128)S(1)}) custom-call(f32[1,8,64]{2,1,0:T(8,128)} %steps_hbm.1, f32[1,64,64]{2,1,0:T(8,128)} %cols_hbm.1, s32[2,1,2]{2,1,0:T(1,128)} %bitcast.9, f32[8,8]{1,0:T(8,128)} %table_hbm.1, ...), custom_call_target="tpu_custom_call" | custom-call | tf_op jit(solution)/shard_map/fetch/pallas_call | solution.py:270
  1.9 2.5 %collective-permute-start.1 = (f32[1,40,128]{2,1,0:T(8,128)S(1)}, f32[1,40,128]{2,1,0:T(8,128)S(1)}, u32[]{:S(2)}, u32[]{:S(2)}) collective-permute-start(f32[1,40,128]{2,1,0:T(8,128)S(1)} %get-tuple-element.25.map_ref), channel_id=1, source_target_pairs={{0,16},{8,24},{16,0},{24,8},{1,17},{9,25},{17,1},{25,9},{2,18},{10... | collective-permute-start | bytes 61448 | tf_op jit(solution)/shard_map/ppermute | solution.py:291
  4.4 0.4 prepare.1
  4.8 0.0 collective-permute-done.vol_ref
  4.8 0.2 halve.1
  5.0 1.1 %shard_map.73.refs_0_ = f32[1040,128]{1,0:T(8,128)S(1)} custom-call(s32[1]{0:T(128)} %bitcast.view_ref, bf16[512,512]{1,0:T(8,128)(2,1)S(1)} %get-tuple-element.20.hi_ref, bf16[512,512]{1,0:T(8,128)(2,1)S(1)} %get-tuple-element.21.lo_ref, bf16[512,512]{1,0:T(8,128)(2,1)S(1)} %get-tuple-element.22.hi_swapped_ref, ...), custom_call_target="tpu_custom_call" | custom-call | flops 1000000000 | bytes 2000000 | tf_op jit(solution)/shard_map/pallas_call | solution.py:319
  6.1 0.1 collective-permute-done.1.map_ref
  6.2 1.1 %shard_map.74 = f32[1040,128]{1,0:T(8,128)S(1)} custom-call(s32[1]{0:T(128)} %bitcast.view_ref, bf16[512,512]{1,0:T(8,128)(2,1)S(1)} %get-tuple-element.20.hi_ref, bf16[512,512]{1,0:T(8,128)(2,1)S(1)} %get-tuple-element.21.lo_ref, bf16[512,512]{1,0:T(8,128)(2,1)S(1)} %get-tuple-element.22.hi_swapped_ref, ...), custom_call_target="tpu_custom_call", output_to_operand_aliasing={{}: (7, {})} | custom-call | flops 1000000000 | bytes 2000000 | tf_op jit(solution)/shard_map/pallas_call | solution.py:319
  7.3 19.7 %all_to_all.10 = f32[16,65,1,128]{3,2,1,0:T(1,128)S(1)} all-to-all(f32[16,65,1,128]{3,2,1,0:T(1,128)S(1)} %bitcast.8), channel_id=1, replica_groups={{21,23,0,2,4,6,16,18,20,22,1,3,5,7,17,19},{29,31,8,10,12,14,24,26,28,30..., dimensions={0} | all-to-all | bytes 1064960 | tf_op jit(solution)/shard_map/all_to_all | solution.py:331
  27.0 1.8 %render.1 = f32[8,8,128]{2,1,0:T(8,128)S(1)} custom-call(f32[1040,128]{1,0:T(8,128)S(1)} %bitcast.7, bf16[128,128]{1,0:T(8,128)(2,1)S(1)} %get-tuple-element.26.maps_hi_ref, bf16[128,128]{1,0:T(8,128)(2,1)S(1)} %get-tuple-element.27.maps_lo_ref, s32[16,128]{1,0:T(8,128)S(1)} %get-tuple-element.28.entry_ref), custom_call_target="tpu_custom_call" | custom-call | tf_op jit(solution)/shard_map/render/pallas_call | solution.py:333
  28.8 8.4 %all_to_all.11.recv_ref = f32[8,8,128]{2,1,0:T(8,128)S(1)} all-to-all(f32[8,8,128]{2,1,0:T(8,128)S(1)} %render.1), channel_id=1, replica_groups={{5,6,7,0,1,2,3,4},{13,14,15,8,9,10,11,12},{21,22,23,16,17,18,19,20},{29..., dimensions={0} | all-to-all | bytes 65536 | tf_op jit(solution)/shard_map/all_to_all | solution.py:341
  37.2 0.7 %unpack.1 = f32[1,3,16,128]{3,2,1,0:T(8,128)} custom-call(f32[8,8,128]{2,1,0:T(8,128)S(1)} %all_to_all.11.recv_ref), custom_call_target="tpu_custom_call" | custom-call | tf_op jit(solution)/shard_map/unpack/pallas_call | solution.py:342
Async XLA Ops:
  0.0 4.8 %collective-permute-start = (f32[4,128,512]{2,1,0:T(8,128)}, f32[4,128,512]{2,1,0:T(8,128)S(1)}, u32[]{:S(2)}, u32[]{:S(2)}) collective-permute-start(f32[4,128,512]{2,1,0:T(8,128)} %vol_hbm.1), channel_id=1, source_target_pairs={{0,8},{8,0},{16,24},{24,16},{1,9},{9,1},{17,25},{25,17},{2,10},{10... | collective-permute-start | bytes 3145736 | tf_op jit(solution)/shard_map/ppermute | solution.py:269
  1.9 4.3 %collective-permute-start.1 = (f32[1,40,128]{2,1,0:T(8,128)S(1)}, f32[1,40,128]{2,1,0:T(8,128)S(1)}, u32[]{:S(2)}, u32[]{:S(2)}) collective-permute-start(f32[1,40,128]{2,1,0:T(8,128)S(1)} %get-tuple-element.25.map_ref), channel_id=1, source_target_pairs={{0,16},{8,24},{16,0},{24,8},{1,17},{9,25},{17,1},{25,9},{2,18},{10... | collective-permute-start | bytes 61448 | tf_op jit(solution)/shard_map/ppermute | solution.py:291

commit v2 on v1

--- a/solution.py
+++ b/solution.py
@@ -22,10 +22,12 @@
     return hi, (x - hi.astype(jnp.float32)).astype(jnp.bfloat16)
 
 
+LOG2E = 1.4426950408889634
+
+
 def softplus(v):
-    e = jnp.exp(-jnp.abs(v))
-    small = e * (1.0 - 0.5 * e)
-    return jnp.maximum(v, 0.0) + jnp.where(e < 1e-4, small, jnp.log(1.0 + e))
+    e = jnp.exp2(jnp.abs(v) * -LOG2E)
+    return jnp.maximum(v, 0.0) + jnp.where(e < 2.0**-12, e, jnp.log(1.0 + e))
 
 
 def fetch_kernel(
@@ -184,7 +186,7 @@
         ) + lax.dot_general(high, maps_lo, NN, preferred_element_type=jnp.float32)
         for m in range(2):
             c = m * SUB + x
-            live = jnp.where(entry_ref[c : c + 1, :] <= brick, step_length, 0.0)
+            live = jnp.where(entry_ref[c : c + 1, :] <= brick, -step_length * LOG2E, 0.0)
             total = jnp.zeros((bricks, rows), jnp.float32)
             before = jnp.ones((bricks, rows), jnp.float32)
             colours = [jnp.zeros((bricks, rows), jnp.float32) for _ in range(3)]
@@ -192,7 +194,7 @@
                 at = (m * steps + s) * bricks
                 v = samples[at : at + bricks]
                 total = total + live * softplus(coef[6] * v + coef[7])
-                after = jnp.exp(-total)
+                after = jnp.exp2(total)
                 weight = before - after
                 before = after
                 for ch in range(3):
@@ -200,7 +202,7 @@
             front = total
             for shift in (1, 2, 4):
                 front = front + jnp.where(brick >= shift, pltpu.roll(front, shift, 0), 0.0)
-            reach = jnp.exp(total - front)
+            reach = jnp.exp2(front - total)
             for ch in range(3):
                 shown[ch][c] = jnp.sum(reach * colours[ch], axis=0, keepdims=True)
     blank = jnp.zeros((LANES // 2 - 3 * columns, rows), jnp.float32)

time: 38.1 us -> 37.8 us (level)
  no operation moved by 1% of the time
where the time goes in v2:
time: 37.8 us; the launch traced here: 37.6 us
  blocking collectives  28.1 us (74%)
  Pallas kernels  6.3 us (17%)
  starting transfers between devices  3.04 us (8%)
    all_to_all x1, blocking collectives, with_kernels(): lax.all_to_all(blocks, ('view', 'depth'), split_axis=0, concat_axis=0, ti...  19.7 us
    all_to_all x1, blocking collectives, with_kernels(): lax.all_to_all(image, 'depth', split_axis=0, concat_axis=0, tiled=True, a...  8.43 us
    ppermute x1, starting transfers between devices, with_kernels(): far = lax.ppermute(own, 'view', [(i, i ^ CORES) for i in range(views)])  2.54 us
    pallas_call x2, Pallas kernels, with_kernels(): pl.pallas_call(functools.partial(send_kernel, order, depth, planes, flip)...  2.24 us
    pallas_call x1, Pallas kernels, with_kernels(): pl.pallas_call(functools.partial(render_kernel, step_length, CORES * plan...  1.44 us
    pallas_call x1, Pallas kernels, with_kernels(): pl.pallas_call(fetch_kernel, out_shape=[jax.ShapeDtypeStruct((1, edge //...  1.36 us
  transfers between devices with their start and end apart: 2, of which 1 were waited for; matrix products, arithmetic and copies ran while one was open for 0% of the time, Pallas kernels for 8%

profile of v2, /device:TPU:0, one launch (start us, length us, event | category | flops | bytes accessed | tf_op | source)
XLA Modules:
  0.0 37.6 jit_solution(159564784084310851)
XLA Ops:
  0.0 0.5 %collective-permute-start = (f32[4,128,512]{2,1,0:T(8,128)}, f32[4,128,512]{2,1,0:T(8,128)S(1)}, u32[]{:S(2)}, u32[]{:S(2)}) collective-permute-start(f32[4,128,512]{2,1,0:T(8,128)} %vol_hbm.1), channel_id=1, source_target_pairs={{0,8},{8,0},{16,24},{24,16},{1,9},{9,1},{17,25},{25,17},{2,10},{10... | collective-permute-start | bytes 3145736 | tf_op jit(solution)/shard_map/ppermute | solution.py:271
  0.5 1.4 %fetch.1 = (f32[1,40,128]{2,1,0:T(8,128)S(1)}, f32[4,128,512]{2,1,0:T(8,128)S(1)}, f32[1,64,64]{2,1,0:T(8,128)S(1)}, s32[1,128,128]{2,1,0:T(8,128)S(1)}, f32[2,128]{1,0:T(2,128)S(1)}) custom-call(f32[1,8,64]{2,1,0:T(8,128)} %steps_hbm.1, f32[1,64,64]{2,1,0:T(8,128)} %cols_hbm.1, s32[2,1,2]{2,1,0:T(1,128)} %bitcast.9, f32[8,8]{1,0:T(8,128)} %table_hbm.1, ...), custom_call_target="tpu_custom_call" | custom-call | tf_op jit(solution)/shard_map/fetch/pallas_call | solution.py:272
  1.9 2.5 %collective-permute-start.1 = (f32[1,40,128]{2,1,0:T(8,128)S(1)}, f32[1,40,128]{2,1,0:T(8,128)S(1)}, u32[]{:S(2)}, u32[]{:S(2)}) collective-permute-start(f32[1,40,128]{2,1,0:T(8,128)S(1)} %get-tuple-element.25.map_ref), channel_id=1, source_target_pairs={{0,16},{8,24},{16,0},{24,8},{1,17},{9,25},{17,1},{25,9},{2,18},{10... | collective-permute-start | bytes 61448 | tf_op jit(solution)/shard_map/ppermute | solution.py:293
  4.4 0.4 prepare.1
  4.8 0.0 collective-permute-done.vol_ref
  4.8 0.2 halve.1
  5.0 1.1 %shard_map.73.refs_0_ = f32[1040,128]{1,0:T(8,128)S(1)} custom-call(s32[1]{0:T(128)} %bitcast.view_ref, bf16[512,512]{1,0:T(8,128)(2,1)S(1)} %get-tuple-element.20.hi_ref, bf16[512,512]{1,0:T(8,128)(2,1)S(1)} %get-tuple-element.21.lo_ref, bf16[512,512]{1,0:T(8,128)(2,1)S(1)} %get-tuple-element.22.hi_swapped_ref, ...), custom_call_target="tpu_custom_call" | custom-call | flops 1000000000 | bytes 2000000 | tf_op jit(solution)/shard_map/pallas_call | solution.py:321
  6.1 0.1 collective-permute-done.1.map_ref
  6.2 1.1 %shard_map.74 = f32[1040,128]{1,0:T(8,128)S(1)} custom-call(s32[1]{0:T(128)} %bitcast.view_ref, bf16[512,512]{1,0:T(8,128)(2,1)S(1)} %get-tuple-element.20.hi_ref, bf16[512,512]{1,0:T(8,128)(2,1)S(1)} %get-tuple-element.21.lo_ref, bf16[512,512]{1,0:T(8,128)(2,1)S(1)} %get-tuple-element.22.hi_swapped_ref, ...), custom_call_target="tpu_custom_call", output_to_operand_aliasing={{}: (7, {})} | custom-call | flops 1000000000 | bytes 2000000 | tf_op jit(solution)/shard_map/pallas_call | solution.py:321
  7.3 19.7 %all_to_all.10 = f32[16,65,1,128]{3,2,1,0:T(1,128)S(1)} all-to-all(f32[16,65,1,128]{3,2,1,0:T(1,128)S(1)} %bitcast.8), channel_id=1, replica_groups={{21,23,0,2,4,6,16,18,20,22,1,3,5,7,17,19},{29,31,8,10,12,14,24,26,28,30..., dimensions={0} | all-to-all | bytes 1064960 | tf_op jit(solution)/shard_map/all_to_all | solution.py:333
  27.0 1.4 %render.1 = f32[8,8,128]{2,1,0:T(8,128)S(1)} custom-call(f32[1040,128]{1,0:T(8,128)S(1)} %bitcast.7, bf16[128,128]{1,0:T(8,128)(2,1)S(1)} %get-tuple-element.26.maps_hi_ref, bf16[128,128]{1,0:T(8,128)(2,1)S(1)} %get-tuple-element.27.maps_lo_ref, s32[16,128]{1,0:T(8,128)S(1)} %get-tuple-element.28.entry_ref), custom_call_target="tpu_custom_call" | custom-call | tf_op jit(solution)/shard_map/render/pallas_call | solution.py:335
  28.5 8.4 %all_to_all.11.recv_ref = f32[8,8,128]{2,1,0:T(8,128)S(1)} all-to-all(f32[8,8,128]{2,1,0:T(8,128)S(1)} %render.1), channel_id=1, replica_groups={{5,6,7,0,1,2,3,4},{13,14,15,8,9,10,11,12},{21,22,23,16,17,18,19,20},{29..., dimensions={0} | all-to-all | bytes 65536 | tf_op jit(solution)/shard_map/all_to_all | solution.py:343
  36.9 0.7 %unpack.1 = f32[1,3,16,128]{3,2,1,0:T(8,128)} custom-call(f32[8,8,128]{2,1,0:T(8,128)S(1)} %all_to_all.11.recv_ref), custom_call_target="tpu_custom_call" | custom-call | tf_op jit(solution)/shard_map/unpack/pallas_call | solution.py:344
Async XLA Ops:
  0.0 4.8 %collective-permute-start = (f32[4,128,512]{2,1,0:T(8,128)}, f32[4,128,512]{2,1,0:T(8,128)S(1)}, u32[]{:S(2)}, u32[]{:S(2)}) collective-permute-start(f32[4,128,512]{2,1,0:T(8,128)} %vol_hbm.1), channel_id=1, source_target_pairs={{0,8},{8,0},{16,24},{24,16},{1,9},{9,1},{17,25},{25,17},{2,10},{10... | collective-permute-start | bytes 3145736 | tf_op jit(solution)/shard_map/ppermute | solution.py:271
  1.9 4.3 %collective-permute-start.1 = (f32[1,40,128]{2,1,0:T(8,128)S(1)}, f32[1,40,128]{2,1,0:T(8,128)S(1)}, u32[]{:S(2)}, u32[]{:S(2)}) collective-permute-start(f32[1,40,128]{2,1,0:T(8,128)S(1)} %get-tuple-element.25.map_ref), channel_id=1, source_target_pairs={{0,16},{8,24},{16,0},{24,8},{1,17},{9,25},{17,1},{25,9},{2,18},{10... | collective-permute-start | bytes 61448 | tf_op jit(solution)/shard_map/ppermute | solution.py:293
